TPU v7x, 32 devices: a whole 2x2x4 slice. The times are simulated.
32 devices in a mesh: lat: 8 (over y, x, core), lev: 4 (over z).
Axes of the slice: x: 2, y: 2, z: 4, core: 2. Of those that a mesh axis runs over, the one named last changes fastest.
Arguments:
- fields: float32 [12, 128, 256, 1024], P(None, 'lev', 'lat'), may hold values from -6 to 6
- legendre: bfloat16 [256, 256, 256], P('lat'), as said below
- owner_counts: int32 [8], replicated, may hold values from 1 to 64, 256 in all
Outputs:
- covariance: float32 [512, 128, 128], P('lat', 'lev')
Inputs may be any that keep to these rules, and one draw needn't show every extreme that they name: `owner_counts`: each owner holds 1 to 64 total wavenumbers, the counts sum to 256, and some owner holds exactly 64. legendre[lat, m, n] is zero where n < m.
All inputs are finite; a program needn't handle non-finite values.
Results may differ from a plain program's by a relative error of at most 0.0038.
Values may be sent and summed in bfloat16 or wider, within the bound.
A program may use at most 192 MiB of HBM per device.

v0:
```python
import math
import jax
import jax.numpy as jnp
from jax import lax
from jax.sharding import PartitionSpec as P


def fourier_table(points, modes):
    places = jnp.arange(points, dtype=jnp.int32)
    orders = jnp.arange(modes, dtype=jnp.int32)
    phase = places[:, None] * orders[None, :] % points
    angle = phase.astype(jnp.float32) * (2.0 * math.pi / points)
    factor = points ** (-0.5)
    return jnp.stack([jnp.cos(angle) * factor, -jnp.sin(angle) * factor], axis=2)


def on_device(fields, legendre, owner_counts):
    members, lev_rows, lat_rows, points = fields.shape
    modes = legendre.shape[1]
    lev_count = lax.axis_size("lev")
    owners = owner_counts.shape[0]
    capacity = 2 * modes // owners
    dft_table = fourier_table(points, modes)
    spectra = jnp.einsum("belx,xmc->lmcbe", fields, dft_table, precision=lax.Precision.HIGHEST)
    spectra = spectra.reshape(lat_rows, modes, 2 * members * lev_rows).astype(jnp.bfloat16)
    collected_rows, transform_table_rows = (
        lax.all_to_all(spectra, "lat", split_axis=1, concat_axis=0, tiled=True),
        lax.all_to_all(legendre, "lat", split_axis=1, concat_axis=0, tiled=True),
    )
    wavenumber_rows = jnp.einsum(
        "dez,det->tez", collected_rows, transform_table_rows, preferred_element_type=jnp.float32
    )
    resident_modes = wavenumber_rows.shape[1]
    shaped = wavenumber_rows.reshape(modes, resident_modes, 2, members, lev_rows)
    anomaly = (shaped - jnp.mean(shaped, axis=3, keepdims=True)).astype(jnp.bfloat16)
    anomaly = anomaly.reshape(modes, resident_modes, 2 * members * lev_rows)
    starts = jnp.cumsum(owner_counts) - owner_counts
    offset = jnp.arange(capacity, dtype=jnp.int32)
    active_flag = offset[None, :] < owner_counts[:, None]
    slot_index = jnp.where(active_flag, starts[:, None] + offset[None, :], 0).reshape(-1)
    slotted = jnp.take(anomaly, slot_index, axis=0)
    slotted = jnp.where(active_flag.reshape(-1)[:, None, None], slotted, jnp.zeros_like(slotted))
    slotted = slotted[None]
    received = lax.all_to_all(
        lax.all_to_all(slotted, "lat", split_axis=1, concat_axis=2, tiled=True),
        "lev",
        split_axis=2,
        concat_axis=0,
        tiled=True,
    )
    mode_share = received.shape[2]
    blocks = received.reshape(lev_count, capacity, mode_share, 2 * members, lev_rows)
    partial_value = jnp.einsum(
        "esaql,fsaqk->selfk", blocks, blocks, preferred_element_type=jnp.float32
    )
    partial_value = partial_value.reshape(capacity, lev_count * lev_rows, lev_count * lev_rows)
    summed = lax.psum_scatter(partial_value, "lev", scatter_dimension=1, tiled=True)
    owner = lax.axis_index("lat")
    wavenumber = starts[owner] + offset
    live_count = owner_counts[owner]
    divisor = ((members - 1) * (2 * wavenumber + 2)).astype(jnp.float32)
    scaled = summed / divisor[:, None, None]
    return jnp.where((offset < live_count)[:, None, None], scaled, jnp.zeros_like(scaled))


def solution(mesh):
    return jax.shard_map(
        on_device,
        mesh=mesh,
        in_specs=(P(None, "lev", "lat", None), P("lat", None, None), P()),
        out_specs=P("lat", "lev", None),
        check_vma=False,
    )
```

profile of v0, /device:TPU:0, one launch (start us, length us, event | category | flops | bytes accessed | tf_op | source)
XLA Modules:
  0.0 1535.5 jit_solution(14930532763259418552)
XLA Ops:
  6.5 6.5 copy.18
  13.0 5.2 all-to-all-start.1
  18.2 4.2 negate_multiply_fusion
  22.4 85.2 %fusion.7 = bf16[256,2,12,32,32]{0,4,3,2,1:T(8,128)(2,1)} fusion(f32[12,32,32,1024]{3,2,1,0:T(8,128)} %param.3, f32[1024,256,1]{1,0,2:T(8,128)S(1)} %get-tuple-element.7, f32[1024,256,1]{1,0,2:T(8,128)S(1)} %get-tuple-element.8), kind=kOutput, calls=%fused_computation.11 | convolution fusion | flops 77316227072 | bytes 65011712 | tf_op jit(solution)/shard_map/belx,xmc->lmcbe/dot_general | solution.py:24
  107.6 18.2 %copy.15 = bf16[32,256,768]{2,0,1:T(8,128)(2,1)} copy(bf16[32,256,768]{1,0,2:T(8,128)(2,1)} %bitcast.76) | data formatting | bytes 25165824 | tf_op jit(solution)/shard_map/convert_element_type | solution.py:25
  125.8 0.0 copy-start
  125.8 0.0 all-to-all-done.1
  125.9 5.5 all-to-all-start
  131.4 0.2 reduce-scatter.2.cloned.1.call-start
  131.6 0.0 copy-done
  131.6 0.2 reduce-window.9
  131.8 0.0 copy-start.2
  131.8 0.1 iota_add_fusion
  131.9 0.4 copy-done.2
  132.3 0.1 select_n.90
  132.4 0.1 add.91
  132.5 0.1 iota_compare_fusion
  132.5 0.1 lt.78
  132.6 4.8 copy.19
  137.4 132.9 %all-to-all-done = bf16[32,256,768]{2,0,1:T(8,128)(2,1)} async-done(((bf16[32,256,768]{2,0,1:T(8,128)(2,1)}), bf16[32,256,768]{2,0,1:T(8,128)(2,1)}, u32[]{:S(2)}, u32[]{:S(2)}) %all-to-all-start) | async-done | bytes 12582944 | tf_op jit(solution)/shard_map/all_to_all | solution.py:27
  270.4 14.1 copy.17
  284.4 20.2 %fusion.5 = f32[32,768,256]{2,1,0:T(8,128)} fusion(bf16[256,32,256]{2,0,1:T(8,128)(2,1)} %bitcast.75, bf16[256,32,768]{2,1,0:T(8,128)(2,1)} %bitcast.71), kind=kOutput, calls=%fused_computation.8 | convolution fusion | flops 3221225472 | bytes 41943040 | tf_op jit(solution)/shard_map/dez,det->tez/dot_general | solution.py:30
  304.6 10.0 reduce_sum.9
  314.7 0.2 broadcast_multiply_fusion
  314.9 15.0 fusion.4
  329.9 16.8 %copy.21 = bf16[256,32,768]{2,1,0:T(8,128)(2,1)} copy(bf16[256,32,768]{0,2,1:T(8,128)(2,1)} %fusion.4) | data formatting | bytes 25165824 | tf_op jit(solution)/shard_map/convert_element_type | solution.py:35
  346.6 20.6 %gather_fusion = bf16[512,32,768]{2,1,0:T(8,128)(2,1)} fusion(bf16[256,32,768]{2,1,0:T(8,128)(2,1)} %copy.21, s32[1024]{0:T(1024)S(1)} %pad_clamp_fusion), kind=kCustom, calls=%fused_computation | custom fusion | bytes 50333696 | tf_op jit(solution)/shard_map/jit(_take)/gather | solution.py:41
  367.2 22.1 %fusion.3 = bf16[1,512,32,768]{3,2,0,1:T(8,128)(2,1)} fusion(bf16[512,32,768]{2,1,0:T(8,128)(2,1)} %gather_fusion, pred[512]{0:T(512)(128)(4,1)S(1)} %compare_and_fusion, pred[512]{0:T(512)(128)(4,1)S(1)} %lt.78), kind=kLoop, calls=%fused_computation.5 | loop fusion | flops 25165824 | bytes 50332672 | tf_op jit(solution)/shard_map/jit(_where)/select_n | solution.py:42
  389.3 278.2 %all_to_all.69 = bf16[1,512,32,768]{3,2,0,1:T(8,128)(2,1)S(1)} all-to-all(bf16[1,512,32,768]{3,2,0,1:T(8,128)(2,1)} %fusion.3), channel_id=1, replica_groups=mesh['lat'=8,'lev'=4] {'lat'}, dimensions={1} | all-to-all | bytes 50331648 | tf_op jit(solution)/shard_map/all_to_all | solution.py:45
  667.5 8.7 copy.23
  676.2 23.2 %copy.24 = bf16[1,64,256,768]{3,1,0,2:T(8,128)(2,1)S(1)} copy(bf16[1,64,256,768]{3,2,1,0:T(8,128)(2,1)} %bitcast.69) | data formatting | bytes 50331648 | tf_op jit(solution)/shard_map/all_to_all | solution.py:45
  699.4 548.4 %all_to_all.70 = bf16[1,64,256,768]{3,1,0,2:T(8,128)(2,1)} all-to-all(bf16[1,64,256,768]{3,1,0,2:T(8,128)(2,1)S(1)} %copy.24), channel_id=1, replica_groups=mesh['lat'=8,'lev'=4] {'lev'}, dimensions={2} | all-to-all | bytes 50331648 | tf_op jit(solution)/shard_map/all_to_all | solution.py:44
  1247.8 23.9 %copy.25 = bf16[1,64,256,768]{3,2,1,0:T(8,128)(2,1)} copy(bf16[1,64,256,768]{3,1,0,2:T(8,128)(2,1)} %all_to_all.70) | data formatting | bytes 50331648 | tf_op jit(solution)/shard_map/all_to_all | solution.py:44
  1271.7 44.6 %copy.26 = bf16[4,1,64,64,768]{3,4,0,2,1:T(8,128)(2,1)} copy(bf16[4,1,64,64,768]{4,3,0,2,1:T(8,128)(2,1)} %bitcast.70) | data formatting | bytes 50331648 | tf_op jit(solution)/shard_map/all_to_all | solution.py:44
  1316.4 50.3 %convolution_bitcast_fusion = f32[64,4,32,4,32]{4,2,3,1,0:T(8,128)} fusion(bf16[4,64,64,24,32,1]{2,4,3,5,0,1:T(8,128)(2,1)} %bitcast.72, bf16[4,64,64,24,32,1]{2,4,3,0,5,1:T(8,128)(2,1)} %bitcast.73), kind=kOutput, calls=%fused_computation.10 | convolution fusion | flops 3221225472 | bytes 54525952 | tf_op jit(solution)/shard_map/esaql,fsaqk->selfk/dot_general | solution.py:53
  1366.6 0.0 copy-start.3
  1366.6 0.0 copy-start.1
  1366.6 14.6 copy.27
  1381.3 0.0 reduce-scatter.2.cloned.1.call-update
  1381.3 0.0 copy-done.3
  1381.3 0.6 dynamic_slice.7
  1381.9 0.0 copy-done.1
  1381.9 0.6 dynamic_slice.6
  1382.5 0.7 multiply_convert_fusion
  1383.2 0.6 iota_compare_fusion.1
  1383.7 141.1 %reduce-scatter.2.cloned.1.call-done = f32[64,32,128]{0,2,1:T(8,128)} async-done(((f32[64,128,128]{0,2,1:T(8,128)}), f32[64,32,128]{0,2,1:T(8,128)}) %reduce-scatter.2.cloned.1.call-update) | async-done | bytes 1048592 | tf_op jit(solution)/shard_map/reduce_scatter | solution.py:57
  1524.8 1.8 divide_select_fusion
  1526.6 1.8 copy.28
  (4 shorter events, 0.0 us)
Async XLA Ops:
  13.0 112.8 %all-to-all-start.1 = ((bf16[32,256,256]{2,0,1:T(8,128)(2,1)}), bf16[32,256,256]{2,0,1:T(8,128)(2,1)}, u32[]{:S(2)}, u32[]{:S(2)}) async-start(bf16[32,256,256]{2,0,1:T(8,128)(2,1)} %copy.18), calls=%async_computation.1 | async-start | bytes 8388608 | tf_op jit(solution)/shard_map/all_to_all | solution.py:28
  125.8 5.8 copy-start
  125.9 144.5 %all-to-all-start = ((bf16[32,256,768]{2,0,1:T(8,128)(2,1)}), bf16[32,256,768]{2,0,1:T(8,128)(2,1)}, u32[]{:S(2)}, u32[]{:S(2)}) async-start(bf16[32,256,768]{2,0,1:T(8,128)(2,1)} %copy.15), calls=%async_computation | async-start | bytes 25165824 | tf_op jit(solution)/shard_map/all_to_all | solution.py:27
  131.4 1393.5 %reduce-scatter.2.cloned.1.call-start = ((), (), s32[]{:S(2)}) async-start(), calls=%async_computation.5 | async-start | bytes 10485760 | tf_op jit(solution)/shard_map/reduce_scatter | solution.py:57
  131.8 0.5 copy-start.2
  1366.6 14.7 copy-start.3
  1366.6 15.3 copy-start.1
Sparse Core Ops, SparseCore 0:
  1381.4 143.3 reduce-scatter.1
where the time goes:
time: 1540 us
  blocking collectives  827 us (54%)
  waiting for transfers between devices  274 us (18%)
  local copies, waits for them, and re-layouts  200 us (13%)
  matrix products  156 us (10%)
  other arithmetic  54.8 us (4%)
    all_to_all x1, blocking collectives, on_device(): lax.all_to_all(lax.all_to_all(slotted, 'lat', split_axis=1, concat_axis=2...  548 us
    all_to_all x1, blocking collectives, on_device(): lax.all_to_all(slotted, 'lat', split_axis=1, concat_axis=2, tiled=True)  278 us
    reduce_scatter x1, waiting for transfers between devices, on_device(): lax.psum_scatter(partial_value, 'lev', scatter_dimension=1, tiled=True)  141 us
    all_to_all x1, waiting for transfers between devices, on_device(): lax.all_to_all(spectra, 'lat', split_axis=1, concat_axis=0, tiled=True)  133 us
    dot_general x1, matrix products, on_device(): jnp.einsum('belx,xmc->lmcbe', fields, dft_table, precision=lax.Precision....  85.2 us
    all_to_all x2, local copies, waits for them, and re-layouts, on_device(): lax.all_to_all(lax.all_to_all(slotted, 'lat', split_axis=1, concat_axis=2...  68.5 us
    dot_general x1, matrix products, on_device(): jnp.einsum('esaql,fsaqk->selfk', blocks, blocks, preferred_element_type=j...  50.3 us
    all_to_all x2, local copies, waits for them, and re-layouts, on_device(): lax.all_to_all(slotted, 'lat', split_axis=1, concat_axis=2, tiled=True)  31.9 us
  transfers between devices with their start and end apart: 3, of which 2 were waited for; matrix products, arithmetic and copies ran while one was open for 8% of the time, Pallas kernels for 0%

commit v1 on v0

--- a/solution.py
+++ b/solution.py
@@ -24,7 +24,12 @@
     spectra = jnp.einsum("belx,xmc->lmcbe", fields, dft_table, precision=lax.Precision.HIGHEST)
     spectra = spectra.reshape(lat_rows, modes, 2 * members * lev_rows).astype(jnp.bfloat16)
     collected_rows, transform_table_rows = (
-        lax.all_to_all(spectra, "lat", split_axis=1, concat_axis=0, tiled=True),
+        jnp.concatenate(
+            jax.lax.all_to_all(
+                jnp.stack(jnp.split(spectra, jax.lax.axis_size("lat"), axis=1), axis=0), "lat", 0, 0
+            ),
+            0,
+        ),
         lax.all_to_all(legendre, "lat", split_axis=1, concat_axis=0, tiled=True),
     )
     wavenumber_rows = jnp.einsum(

time: 1540 us -> 1620 us (1.052)
  local copies, waits for them, and re-layouts: 200 us -> 276 us
    unnamed x9 -> x28, local copies, waits for them, and re-layouts: 6.95 us -> 81.9 us
    split x0 -> x1, local copies, waits for them, and re-layouts: none -> 32.3 us  [on_device(): jnp.split(spectra, jax.lax.axis_size('lat'), axis=1)]
    convert_element_type x1 -> x0, local copies, waits for them, and re-layouts: 18.2 us -> none  [on_device(): spectra.reshape(lat_rows, modes, 2 * members * lev_rows)]
  transfers between devices with their start and end apart: 3 -> 3, of which waited for: 2 -> 2; matrix products, arithmetic and copies ran while one was open for 8% -> 13% of each run, Pallas kernels for 0% -> 0%
where the time goes in v1:
time: 1620 us; the launch traced here: 1610 us
  blocking collectives  826 us (51%)
  local copies, waits for them, and re-layouts  276 us (17%)
  waiting for transfers between devices  274 us (17%)
  matrix products  156 us (10%)
  other arithmetic  54.9 us (3%)
    all_to_all x1, blocking collectives, on_device(): lax.all_to_all(lax.all_to_all(slotted, 'lat', split_axis=1, concat_axis=2...  548 us
    all_to_all x1, blocking collectives, on_device(): lax.all_to_all(slotted, 'lat', split_axis=1, concat_axis=2, tiled=True)  278 us
    reduce_scatter x1, waiting for transfers between devices, on_device(): lax.psum_scatter(partial_value, 'lev', scatter_dimension=1, tiled=True)  141 us
    all_to_all x1, waiting for transfers between devices, on_device(): jax.lax.all_to_all(jnp.stack(jnp.split(spectra, jax.lax.axis_size('lat'),...  133 us
    dot_general x1, matrix products, on_device(): jnp.einsum('belx,xmc->lmcbe', fields, dft_table, precision=lax.Precision....  85 us
    unnamed x28, local copies, waits for them, and re-layouts  81.9 us
    all_to_all x2, local copies, waits for them, and re-layouts, on_device(): lax.all_to_all(lax.all_to_all(slotted, 'lat', split_axis=1, concat_axis=2...  68.5 us
    dot_general x1, matrix products, on_device(): jnp.einsum('esaql,fsaqk->selfk', blocks, blocks, preferred_element_type=j...  50.2 us
  transfers between devices with their start and end apart: 3, of which 2 were waited for; matrix products, arithmetic and copies ran while one was open for 13% of the time, Pallas kernels for 0%

profile of v1, /device:TPU:0, one launch (start us, length us, event | category | flops | bytes accessed | tf_op | source)
XLA Modules:
  0.0 1611.3 jit_solution(8057386641509092538)
XLA Ops:
  6.5 6.5 copy.29
  13.1 5.2 all-to-all-start.1
  18.3 4.2 negate_multiply_fusion
  22.4 85.0 %fusion.7 = bf16[256,2,12,32,32]{0,4,3,2,1:T(8,128)(2,1)} fusion(f32[12,32,32,1024]{3,2,1,0:T(8,128)} %param.3, f32[1024,256,1]{1,0,2:T(8,128)S(1)} %get-tuple-element.15, f32[1024,256,1]{1,0,2:T(8,128)S(1)} %get-tuple-element.16), kind=kOutput, calls=%fused_computation.11 | convolution fusion | flops 77316227072 | bytes 65011712 | tf_op jit(solution)/shard_map/belx,xmc->lmcbe/dot_general | solution.py:24
  107.4 32.3 %fusion.19 = (bf16[32,32,768]{1,0,2:T(8,128)(2,1)}, bf16[32,32,768]{1,0,2:T(8,128)(2,1)}, bf16[32,32,768]{1,0,2:T(8,128)(2,1)}, bf16[32,32,768]{1,0,2:T(8,128)(2...) fusion(bf16[32,256,768]{1,0,2:T(8,128)(2,1)} %bitcast.81), kind=kLoop, calls=%fused_computation.47 | loop fusion | bytes 25165824 | tf_op jit(solution)/shard_map/split | solution.py:29
  139.7 7.8 copy.44
  147.4 7.7 copy.45
  155.2 7.7 copy.46
  162.9 7.7 copy.47
  170.6 7.8 copy.48
  178.4 7.7 copy.49
  186.1 6.9 copy.50
  193.0 6.9 copy.51
  200.0 2.8 bitcast_dynamic-update-slice_fusion.7
  202.8 2.7 bitcast_dynamic-update-slice_fusion.6
  205.4 2.7 bitcast_dynamic-update-slice_fusion.5
  208.1 2.7 bitcast_dynamic-update-slice_fusion.4
  210.8 1.2 bitcast_dynamic-update-slice_fusion.3
  212.0 1.3 bitcast_dynamic-update-slice_fusion.2
  213.4 1.3 bitcast_dynamic-update-slice_fusion.1
  214.6 1.3 bitcast_dynamic-update-slice_fusion
  215.9 5.5 all-to-all-start
  221.5 0.2 reduce-window.9
  221.8 0.4 copy-done.4
  222.5 4.8 copy.30
  227.3 133.1 %all-to-all-done = bf16[8,32,32,768]{3,2,1,0:T(8,128)(2,1)} async-done(((bf16[8,32,32,768]{3,2,1,0:T(8,128)(2,1)}), bf16[8,32,32,768]{3,2,1,0:T(8,128)(2,1)}, u32[]{:S(2)}, u32[]{:S(2)}) %all-to-all-start) | async-done | bytes 12582944 | tf_op jit(solution)/shard_map/all_to_all | solution.py:28
  360.4 20.6 %fusion.5 = f32[32,768,256]{2,1,0:T(8,128)} fusion(bf16[256,32,256]{2,0,1:T(8,128)(2,1)} %bitcast.88, bf16[256,32,768]{2,1,0:T(8,128)(2,1)} %bitcast.17), kind=kOutput, calls=%fused_computation.8 | convolution fusion | flops 3221225472 | bytes 41943040 | tf_op jit(solution)/shard_map/dez,det->tez/dot_general | solution.py:35
  381.0 10.0 reduce_sum.9
  391.0 0.2 broadcast_multiply_fusion
  391.2 14.9 fusion.4
  406.1 16.8 %copy.32 = bf16[256,32,768]{2,1,0:T(8,128)(2,1)} copy(bf16[256,32,768]{0,2,1:T(8,128)(2,1)} %fusion.4) | data formatting | bytes 25165824 | tf_op jit(solution)/shard_map/convert_element_type | solution.py:40
  422.9 20.4 %gather_fusion = bf16[512,32,768]{2,1,0:T(8,128)(2,1)} fusion(bf16[256,32,768]{2,1,0:T(8,128)(2,1)} %copy.32, s32[1024]{0:T(1024)S(1)} %pad_clamp_fusion), kind=kCustom, calls=%fused_computation | custom fusion | bytes 50333696 | tf_op jit(solution)/shard_map/jit(_take)/gather | solution.py:46
  443.3 22.1 %fusion.3 = bf16[1,512,32,768]{3,2,0,1:T(8,128)(2,1)} fusion(bf16[512,32,768]{2,1,0:T(8,128)(2,1)} %gather_fusion, pred[512]{0:T(512)(128)(4,1)S(1)} %compare_and_fusion, pred[512]{0:T(512)(128)(4,1)S(1)} %lt.78), kind=kLoop, calls=%fused_computation.5 | loop fusion | flops 25165824 | bytes 50332672 | tf_op jit(solution)/shard_map/jit(_where)/select_n | solution.py:47
  465.4 278.4 %all_to_all.56 = bf16[1,512,32,768]{3,2,0,1:T(8,128)(2,1)S(1)} all-to-all(bf16[1,512,32,768]{3,2,0,1:T(8,128)(2,1)} %fusion.3), channel_id=1, replica_groups=mesh['lat'=8,'lev'=4] {'lat'}, dimensions={1} | all-to-all | bytes 50331648 | tf_op jit(solution)/shard_map/all_to_all | solution.py:50
  743.8 8.7 copy.34
  752.5 23.2 %copy.35 = bf16[1,64,256,768]{3,1,0,2:T(8,128)(2,1)S(1)} copy(bf16[1,64,256,768]{3,2,1,0:T(8,128)(2,1)} %bitcast.83) | data formatting | bytes 50331648 | tf_op jit(solution)/shard_map/all_to_all | solution.py:50
  775.8 548.1 %all_to_all.57 = bf16[1,64,256,768]{3,1,0,2:T(8,128)(2,1)} all-to-all(bf16[1,64,256,768]{3,1,0,2:T(8,128)(2,1)S(1)} %copy.35), channel_id=1, replica_groups=mesh['lat'=8,'lev'=4] {'lev'}, dimensions={2} | all-to-all | bytes 50331648 | tf_op jit(solution)/shard_map/all_to_all | solution.py:49
  1323.9 23.9 %copy.36 = bf16[1,64,256,768]{3,2,1,0:T(8,128)(2,1)} copy(bf16[1,64,256,768]{3,1,0,2:T(8,128)(2,1)} %all_to_all.57) | data formatting | bytes 50331648 | tf_op jit(solution)/shard_map/all_to_all | solution.py:49
  1347.7 44.6 %copy.37 = bf16[4,1,64,64,768]{3,4,0,2,1:T(8,128)(2,1)} copy(bf16[4,1,64,64,768]{4,3,0,2,1:T(8,128)(2,1)} %bitcast.84) | data formatting | bytes 50331648 | tf_op jit(solution)/shard_map/all_to_all | solution.py:49
  1392.3 50.2 %convolution_bitcast_fusion = f32[64,4,32,4,32]{4,2,3,1,0:T(8,128)} fusion(bf16[4,64,64,24,32,1]{2,4,3,5,0,1:T(8,128)(2,1)} %bitcast.85, bf16[4,64,64,24,32,1]{2,4,3,0,5,1:T(8,128)(2,1)} %bitcast.86), kind=kOutput, calls=%fused_computation.10 | convolution fusion | flops 3221225472 | bytes 54525952 | tf_op jit(solution)/shard_map/esaql,fsaqk->selfk/dot_general | solution.py:58
  1442.5 14.7 copy.38
  1457.2 0.6 dynamic_slice.7
  1457.8 0.7 dynamic_slice.6
  1458.5 0.7 multiply_convert_fusion
  1459.1 0.7 iota_compare_fusion.1
  1459.8 140.9 %reduce-scatter.2.cloned.1.call-done = f32[64,32,128]{0,2,1:T(8,128)} async-done(((f32[64,128,128]{0,2,1:T(8,128)}), f32[64,32,128]{0,2,1:T(8,128)}) %reduce-scatter.2.cloned.1.call-update) | async-done | bytes 1048592 | tf_op jit(solution)/shard_map/reduce_scatter | solution.py:62
  1600.7 1.8 divide_select_fusion
  1602.5 1.8 copy.39
  (23 shorter events, 0.5 us)
Async XLA Ops:
  13.1 202.8 %all-to-all-start.1 = ((bf16[32,256,256]{2,0,1:T(8,128)(2,1)}), bf16[32,256,256]{2,0,1:T(8,128)(2,1)}, u32[]{:S(2)}, u32[]{:S(2)}) async-start(bf16[32,256,256]{2,0,1:T(8,128)(2,1)} %copy.29), calls=%async_computation.1 | async-start | bytes 8388608 | tf_op jit(solution)/shard_map/all_to_all | solution.py:33
  199.9 10.8 copy-start.1
  200.0 12.1 copy-start
  215.9 5.6 copy-start.2
  215.9 144.5 %all-to-all-start = ((bf16[8,32,32,768]{3,2,1,0:T(8,128)(2,1)}), bf16[8,32,32,768]{3,2,1,0:T(8,128)(2,1)}, u32[]{:S(2)}, u32[]{:S(2)}) async-start(bf16[8,32,32,768]{3,2,1,0:T(8,128)(2,1)} %bitcast_dynamic-update-slice_fusion), calls=%async_computation | async-start | bytes 25165824 | tf_op jit(solution)/shard_map/all_to_all | solution.py:28
  221.4 1379.3 %reduce-scatter.2.cloned.1.call-start = ((), (), s32[]{:S(2)}) async-start(), calls=%async_computation.5 | async-start | bytes 10485760 | tf_op jit(solution)/shard_map/reduce_scatter | solution.py:62
  221.7 0.5 copy-start.4
  1442.5 14.7 copy-start.5
  1442.5 15.3 copy-start.3
Sparse Core Ops, SparseCore 0:
  1457.3 143.3 reduce-scatter.1
